TPU v7x, 32 devices: a whole 2x2x4 slice. The times are simulated.
32 devices in a mesh: samp: 8 (over y, x, core), par: 4 (over z).
Axes of the slice: x: 2, y: 2, z: 4, core: 2. Of those that a mesh axis runs over, the one named last changes fastest.
Arguments:
- log_derivs: bfloat16 [512, 262144], P('samp', 'par')
- energies: float32 [512, 8], P('samp'), may hold values from -6 to 6
- nys_rows: int32 [8, 8], P('samp'), may hold values from 0 to 63, as said below
Outputs:
- update: float32 [262144, 8], P('par')
- solution: float32 [512, 8], P('samp')
Inputs may be any that keep to these rules, and one draw needn't show every extreme that they name: `nys_rows`: each row holds 8 different local sample numbers of that group.
All inputs are finite; a program needn't handle non-finite values.
Results may differ from a plain program's by a relative error of at most 0.014.
Values may be sent and summed in bfloat16 or wider, within the bound.
A program may use at most 128 MiB of HBM per device.

v0:
```python
import math

import jax
import jax.numpy as jnp
from jax import lax
from jax.sharding import PartitionSpec as P

ITERS = 2


damping = 0.5


def factor_solve(factor, right):
    middle = lax.linalg.triangular_solve(factor, right, left_side=True, lower=True)
    return lax.linalg.triangular_solve(factor, middle, left_side=True, lower=True, transpose_a=True)


def small_solve(matrix, right):
    return factor_solve(jnp.linalg.cholesky(matrix), right)


def hdot(left, right):
    return jnp.dot(left, right, precision=lax.Precision.HIGHEST)


def gram_body(log_derivs, energies, nys_rows):
    samp_rows = log_derivs.shape[0]
    groups = lax.axis_size("samp")
    total_rows = samp_rows * groups
    total_cols = log_derivs.shape[1] * lax.axis_size("par")
    slab = lax.all_to_all(log_derivs, "samp", split_axis=1, concat_axis=0, tiled=True)
    widened = slab.astype(jnp.float32)
    col_mean = jnp.sum(widened, axis=0) / total_rows
    centered = ((widened - col_mean) * (1.0 / math.sqrt(total_cols))).astype(jnp.bfloat16)
    gram = lax.psum(
        jnp.einsum("rc,kc->rk", centered, centered, preferred_element_type=jnp.float32),
        ("samp", "par"),
    )
    all_energies = lax.all_gather(energies, "samp", axis=0, tiled=True)
    all_picks = lax.all_gather(nys_rows, "samp", axis=0, tiled=True)
    selected = (jnp.arange(groups, dtype=jnp.int32)[:, None] * samp_rows + all_picks).reshape(-1)
    sketch = jnp.take(gram, selected, axis=1)
    core_block = jnp.take(sketch, selected, axis=0)
    factor = jnp.linalg.cholesky(damping * core_block + hdot(sketch.T, sketch))

    def precondition(residual):
        coeffs = factor_solve(factor, hdot(sketch.T, residual))
        result = (residual - hdot(sketch, coeffs)) / damping
        return (result, hdot(result.T, residual))

    solution = jnp.zeros(all_energies.shape, jnp.float32)
    residual = all_energies
    precond_res, inner_prev = precondition(residual)
    direction = precond_res
    for iteration in range(ITERS):
        rounded = direction.astype(jnp.bfloat16).astype(jnp.float32)
        image_k = hdot(gram, rounded) + damping * direction
        curvature = hdot(direction.T, image_k)
        alpha_k = small_solve(curvature, inner_prev)
        solution = solution + hdot(direction, alpha_k)
        if iteration + 1 < ITERS:
            residual = residual - hdot(image_k, alpha_k)
            precond_res, inner_next = precondition(residual)
            beta_k = small_solve(inner_prev, inner_next)
            direction = precond_res + hdot(direction, beta_k)
            inner_prev = inner_next
    rounded_sol = solution.astype(jnp.bfloat16)
    local_update = jnp.einsum(
        "rc,rv->cv", centered, rounded_sol, preferred_element_type=jnp.float32
    )
    update = lax.all_gather(local_update.astype(jnp.bfloat16), "samp", axis=0, tiled=True).astype(
        local_update.dtype
    )
    start = lax.axis_index("samp") * samp_rows
    return (update, lax.dynamic_slice_in_dim(solution, start, samp_rows, 0))


def body(log_derivs, energies, nys_rows):
    update, solution = gram_body(log_derivs, energies, nys_rows)
    return (update, solution)


def solution(mesh):
    return jax.shard_map(
        body,
        mesh=mesh,
        in_specs=(P("samp", "par"), P("samp", None), P("samp", None)),
        out_specs=(P("par", None), P("samp", None)),
        check_vma=False,
    )
```

profile of v0, /device:TPU:0, one launch (start us, length us, event | category | flops | bytes accessed | tf_op | source)
XLA Modules:
  0.0 351.4 jit_solution(1456690422608163181)
XLA Ops:
  7.2 7.6 %copy.62 = bf16[8,8,8,8192]{3,2,0,1:T(8,128)(2,1)} copy(bf16[8,8,8,8192]{3,2,1,0:T(8,128)(2,1)} %bitcast.122) | data formatting | bytes 16777216 | tf_op jit(solution)/shard_map/all_to_all | solution.py:32
  14.8 5.3 %all-to-all-start = ((bf16[64,8,8192]{2,0,1:T(8,128)(2,1)}), bf16[64,8,8192]{2,0,1:T(8,128)(2,1)}, u32[]{:S(2)}, u32[]{:S(2)}) async-start(bf16[64,8,8192]{2,0,1:T(8,128)(2,1)} %bitcast.121), calls=%async_computation | async-start | bytes 16777216 | tf_op jit(solution)/shard_map/all_to_all | solution.py:32
  20.1 97.4 %all-gather.1 = s32[8,1,8]{2,1,0:T(1,128)S(1)} all-gather(s32[1,1,8]{2,1,0:T(1,128)S(1)} %bitcast.126), channel_id=1, replica_groups=mesh['samp'=8,'par'=4] {'samp'}, dimensions={0}, use_global_device_ids=true | all-gather | bytes 288 | tf_op jit(solution)/shard_map/all_gather | solution.py:41
  117.7 8.3 %all-gather = f32[8,64,8]{1,2,0:T(8,128)S(1)} all-gather(f32[1,64,8]{1,2,0:T(8,128)S(1)} %bitcast.125), channel_id=1, replica_groups=mesh['samp'=8,'par'=4] {'samp'}, dimensions={0}, use_global_device_ids=true | all-gather | bytes 18432 | tf_op jit(solution)/shard_map/all_gather | solution.py:40
  126.1 5.5 %convert_reduce_fusion = f32[8192]{0:T(1024)S(1)} fusion(bf16[64,8,8192]{2,0,1:T(8,128)(2,1)} %all-to-all-done), kind=kLoop, calls=%fused_computation.8 | loop fusion | flops 8380416 | bytes 8421376 | tf_op jit(solution)/shard_map/reduce_sum | solution.py:34
  131.6 8.9 %multiply_convert_fusion = bf16[64,8,8192]{2,0,1:T(8,128)(2,1)} fusion(bf16[64,8,8192]{2,0,1:T(8,128)(2,1)} %all-to-all-done, f32[8192]{0:T(1024)S(1)} %broadcast_multiply_fusion), kind=kLoop, calls=%fused_computation.5 | loop fusion | flops 16777216 | bytes 16809984 | tf_op jit(solution)/shard_map/convert.2
  140.5 11.3 %fusion.73 = f32[512,512]{1,0:T(8,128)} fusion(bf16[512,8192]{1,0:T(8,128)(2,1)} %bitcast.123), kind=kOutput, calls=%fused_computation.118 | convolution fusion | flops 4294967296 | bytes 9437184 | tf_op jit(solution)/shard_map/rc,kc->rk/dot_general | solution.py:37
  152.0 8.9 %fusion.1 = bf16[512,8192]{1,0:T(8,128)(2,1)} fusion(bf16[64,8,8192]{2,0,1:T(8,128)(2,1)} %all-to-all-done, f32[8192]{0:T(1024)S(1)} %broadcast_multiply_fusion), kind=kLoop, calls=%fused_computation.4 | loop fusion | flops 16777216 | bytes 16809984 | tf_op jit(solution)/shard_map/convert_element_type | solution.py:35
  160.9 122.7 %all-reduce.2.cloned.1.call-done = f32[512,512]{1,0:T(8,128)} async-done(((f32[512,512]{1,0:T(8,128)}), f32[512,512]{1,0:T(8,128)}) %all-reduce.2.cloned.1.call-update) | async-done | bytes 1048592 | tf_op jit(solution)/shard_map/psum | solution.py:36
  283.6 1.6 copy.48
  285.2 0.7 gather_fusion
  287.2 5.8 %cholesky.33 = f32[64,64]{1,0:T(8,128)S(1)} custom-call(f32[64,64]{1,0:T(8,128)S(1)} %fusion.29), custom_call_target="Cholesky" | custom-call | tf_op jit(solution)/shard_map/jit(cholesky)/cholesky | solution.py:45
  293.7 0.7 fusion.20
  294.4 4.9 %custom-call.24 = f32[1,64,64]{1,2,0:T(8,128)S(1)} custom-call(f32[1,64,64]{2,1,0:T(8,128)S(1)} %fusion.20), custom_call_target="InvertDiagBlocksLowerTriangular" | custom-call | tf_op jit(solution)/shard_map/triangular_solve/custom-call.3 | solution.py:16
  300.4 1.8 convolution_add_fusion.4
  302.4 0.7 cholesky.94
  303.8 0.6 fusion.44
  305.8 0.7 cholesky.105
  307.3 0.6 fusion.45
  310.9 0.7 cholesky.116
  314.2 5.2 %convolution_convert_fusion = bf16[8192,8]{0,1:T(8,128)(2,1)} fusion(bf16[512,8192]{1,0:T(8,128)(2,1)} %fusion.1, f32[512,8]{0,1:T(8,128)S(1)} %convolution_add_fusion.1), kind=kOutput, calls=%fused_computation.6 | convolution fusion | flops 67178496 | bytes 8536064 | tf_op jit(solution)/shard_map/rc,rv->cv/dot_general | solution.py:69
  319.4 0.7 constant_dynamic-slice_fusion
  320.1 21.8 %all-gather.4.cloned.1.call-done = bf16[65536,8]{0,1:T(8,128)(2,1)} async-done(((bf16[8192,8]{0,1:T(8,128)(2,1)}), bf16[65536,8]{0,1:T(8,128)(2,1)}) %all-gather.4.cloned.1.call-update) | async-done | bytes 1048592 | tf_op jit(solution)/shard_map/all_gather | solution.py:72
  341.9 2.7 convert_element_type.49
  (68 shorter events, 12.2 us)
Async XLA Ops:
  14.8 5.4 %copy-start.2 = (s32[1,8]{1,0:T(1,128)S(1)}, s32[1,8]{1,0:T(1,128)}, u32[]{:S(2)}) copy-start(s32[1,8]{1,0:T(1,128)} %param.14) | copy-start | bytes 100
  14.8 103.0 %copy-start.1 = (f32[64,8]{0,1:T(8,128)S(1)}, f32[64,8]{0,1:T(8,128)}, u32[]{:S(2)}) copy-start(f32[64,8]{0,1:T(8,128)} %param.13) | copy-start | bytes 6148
  14.8 111.4 %all-to-all-start = ((bf16[64,8,8192]{2,0,1:T(8,128)(2,1)}), bf16[64,8,8192]{2,0,1:T(8,128)(2,1)}, u32[]{:S(2)}, u32[]{:S(2)}) async-start(bf16[64,8,8192]{2,0,1:T(8,128)(2,1)} %bitcast.121), calls=%async_computation | async-start | bytes 16777216 | tf_op jit(solution)/shard_map/all_to_all | solution.py:32
  20.1 263.5 %all-reduce.2.cloned.1.call-start = ((), (), s32[]{:S(2)}) async-start(), calls=%async_computation.1 | async-start | bytes 2097152 | tf_op jit(solution)/shard_map/psum | solution.py:36
  151.8 190.1 %all-gather.4.cloned.1.call-start = ((), (), s32[]{:S(2)}) async-start(), calls=%async_computation.2 | async-start | bytes 1179648 | tf_op jit(solution)/shard_map/all_gather | solution.py:72
  283.6 26.5 %copy-start = (f32[512,512]{1,0:T(8,128)S(1)}, f32[512,512]{1,0:T(8,128)}, u32[]{:S(2)}) copy-start(f32[512,512]{1,0:T(8,128)} %all-reduce.2.cloned.1.call-done) | copy-start | bytes 3145732
Sparse Core Ops, SparseCore 0:
  151.9 131.6 all-reduce.1
  319.6 22.3 all-gather.3
where the time goes:
time: 352 us; the launch traced here: 351 us
  waiting for transfers between devices  145 us (41%)
  blocking collectives  106 us (30%)
  other arithmetic  46.2 us (13%)
  matrix products  23.4 us (7%)
  between operations  14.2 us (4%)
  local copies, waits for them, and re-layouts  11.8 us (3%)
  starting transfers between devices  5.59 us (2%)
    psum x1, waiting for transfers between devices, gram_body(): lax.psum(jnp.einsum('rc,kc->rk', centered, centered, preferred_element_ty...  123 us
    all_gather x1, blocking collectives, gram_body(): all_picks = lax.all_gather(nys_rows, 'samp', axis=0, tiled=True)  97.4 us
    all_gather x1, waiting for transfers between devices, gram_body(): lax.all_gather(local_update.astype(jnp.bfloat16), 'samp', axis=0, tiled=T...  21.8 us
    dot_general x1, matrix products, gram_body(): jnp.einsum('rc,kc->rk', centered, centered, preferred_element_type=jnp.fl...  11.3 us
    another operation x8, other arithmetic, factor_solve(): lax.linalg.triangular_solve(factor, middle, left_side=True, lower=True, t...  9.37 us
    another operation x1, other arithmetic  8.89 us
    convert_element_type x1, other arithmetic, gram_body(): ((widened - col_mean) * (1.0 / math.sqrt(total_cols))).astype(jnp.bfloat16)  8.89 us
    all_gather x1, blocking collectives, gram_body(): all_energies = lax.all_gather(energies, 'samp', axis=0, tiled=True)  8.27 us
  transfers between devices with their start and end apart: 3, of which 2 were waited for; matrix products, arithmetic and copies ran while one was open for 3% of the time, Pallas kernels for 0%

commit v1 on v0

v1 whole, which is shorter than its diff:
```python
import functools
import math

import jax
import jax.numpy as jnp
from jax import lax
from jax.experimental import pallas as pl
from jax.experimental.pallas import tpu as pltpu
from jax.sharding import PartitionSpec as P

ITERS = 2


damping = 0.5

MESH = pl.DeviceIdType.MESH


def factor_solve(factor, right):
    middle = lax.linalg.triangular_solve(factor, right, left_side=True, lower=True)
    return lax.linalg.triangular_solve(factor, middle, left_side=True, lower=True, transpose_a=True)


def small_solve(matrix, right):
    return factor_solve(jnp.linalg.cholesky(matrix), right)


def hdot(left, right):
    return jnp.dot(left, right, precision=lax.Precision.HIGHEST)


def greet(peers):
    barrier = pltpu.get_barrier_semaphore()
    for peer in peers:
        pl.semaphore_signal(barrier, inc=1, device_id=peer, device_id_type=MESH)
    pl.semaphore_wait(barrier, len(peers))


def remote(src, dst, send, recv, peer):
    return pltpu.make_async_remote_copy(
        src_ref=src, dst_ref=dst, send_sem=send, recv_sem=recv, device_id=peer, device_id_type=MESH
    )


def gather_kernel(n, total_rows, sums_ref, aux_ref, chosen_ref, mean_ref, aux_out, rows_out,
                  land, own, s1, r1, s2, r2, s3, r3, s4, r4, s5, r5, local):
    me, col = lax.axis_index("samp"), lax.axis_index("par")
    at = [lax.rem(me + k, n) for k in range(n)]
    back = [lax.rem(me + n - k, n) for k in range(n)]
    peer = [(at[k], col) for k in range(n)]
    pair = jnp.bitwise_xor(me, 1)
    greet(peer[1:])
    scatter = [remote(sums_ref.at[at[k]], land.at[k], s1.at[k], r1.at[k], peer[k]) for k in range(1, n)]
    for copy in scatter:
        copy.start()
    auxes = [remote(aux_ref, aux_out.at[me], s2.at[k], r2.at[k], peer[k]) for k in range(1, n)]
    for copy in auxes:
        copy.start()
    mine = pltpu.make_async_copy(aux_ref, aux_out.at[me], local.at[0])
    mine.start()
    keep = pltpu.make_async_copy(chosen_ref, rows_out.at[me], local.at[1])
    keep.start()
    total = sums_ref[me]
    for k in range(1, n):
        scatter[k - 1].wait_recv()
        total = total + land[k]
    own[...] = total / total_rows
    mean_ref[me] = own[...]
    spread = [remote(own, mean_ref.at[me], s3.at[k], r3.at[k], peer[k]) for k in range(1, n)]
    for copy in spread:
        copy.start()
    far = [remote(chosen_ref, rows_out.at[me], s4.at[k], r4.at[k], peer[k]) for k in range(2, n, 2)]
    for copy in far:
        copy.start()
    over = [remote(chosen_ref, rows_out.at[me], s5.at[0], r5.at[0], (pair, col))]
    over[0].start()
    for i, k in enumerate(range(2, n, 2)):
        remote(
            chosen_ref, rows_out.at[back[k]], s4.at[k], r4.at[k], peer[k]).wait_recv()
        step = remote(rows_out.at[back[k]], rows_out.at[back[k]], s5.at[k], r5.at[k], (pair, col))
        step.start()
        over.append(step)
    for i, k in enumerate(range(0, n, 2)):
        source = lax.rem(pair + n - k, n)
        remote(chosen_ref, rows_out.at[source], s5.at[k], r5.at[k], (pair, col)).wait_recv()
    for k in range(1, n):
        remote(aux_ref, aux_out.at[back[k]], s2.at[k], r2.at[k], peer[k]).wait_recv()
        remote(own, mean_ref.at[back[k]], s3.at[k], r3.at[k], peer[k]).wait_recv()
    for copy in scatter + auxes + spread + far + over:
        copy.wait_send()
    mine.wait()
    keep.wait()


def gather_rows(sums, aux, chosen, n, total_rows, ident):
    dma = lambda: pltpu.SemaphoreType.DMA((n,))
    vmem = pl.BlockSpec(memory_space=pltpu.VMEM)
    slab = sums.shape[-1]
    return pl.pallas_call(
        functools.partial(gather_kernel, n, total_rows),
        out_shape=(
            jax.ShapeDtypeStruct(sums.shape, jnp.float32),
            jax.ShapeDtypeStruct((n,) + aux.shape, jnp.float32),
            jax.ShapeDtypeStruct((n,) + chosen.shape, chosen.dtype),
        ),
        in_specs=[vmem, vmem, vmem],
        out_specs=(vmem, vmem, vmem),
        scratch_shapes=[
            pltpu.VMEM(sums.shape, jnp.float32),
            pltpu.VMEM((1, slab), jnp.float32),
        ] + [dma() for _ in range(10)] + [pltpu.SemaphoreType.DMA((2,))],
        compiler_params=pltpu.CompilerParams(
            collective_id=ident, has_side_effects=True, vmem_limit_bytes=48 * 2**20
        ),
    )(sums, aux, chosen)


def spread_kernel(n, p, part_ref, out_ref, land, own, s1, r1, s2, r2):
    me, col = lax.axis_index("samp"), lax.axis_index("par")
    flat, size = me * p + col, n * p
    barrier = pltpu.get_barrier_semaphore()

    def place(k):
        there = lax.rem(flat + k, size)
        return (there // p, lax.rem(there, p))

    @pl.loop(1, size)
    def _(k):
        pl.semaphore_signal(barrier, inc=1, device_id=place(k), device_id_type=MESH)

    pl.semaphore_wait(barrier, size - 1)
    sums = []
    for k in range(1, p):
        there = lax.rem(col + k, p)
        sums.append(remote(part_ref.at[there], land.at[k], s1.at[k], r1.at[k], (me, there)))
        sums[-1].start()
    total = part_ref[col]
    for k in range(1, p):
        sums[k - 1].wait_recv()
        total = total + land[k]
    own[...] = total
    out_ref[flat] = total

    def hop(k, slot):
        return remote(own, out_ref.at[slot], s2.at[k], r2.at[k], place(k))

    @pl.loop(1, size)
    def _(k):
        hop(k, flat).start()

    @pl.loop(1, size)
    def _(k):
        hop(k, lax.rem(flat + size - k, size)).wait_recv()

    @pl.loop(1, size)
    def _(k):
        hop(k, flat).wait_send()

    for copy in sums:
        copy.wait_send()


def sum_and_spread(part, n, p, ident):
    rows, width = part.shape
    cut = part.reshape(p, rows // p, width)
    vmem = pl.BlockSpec(memory_space=pltpu.VMEM)
    out = pl.pallas_call(
        functools.partial(spread_kernel, n, p),
        out_shape=jax.ShapeDtypeStruct((n * p, rows // p, width), jnp.float32),
        in_specs=[vmem],
        out_specs=vmem,
        scratch_shapes=[
            pltpu.VMEM(cut.shape, jnp.float32),
            pltpu.VMEM(cut.shape[1:], jnp.float32),
            pltpu.SemaphoreType.DMA((p,)),
            pltpu.SemaphoreType.DMA((p,)),
            pltpu.SemaphoreType.DMA((n * p,)),
            pltpu.SemaphoreType.DMA((n * p,)),
        ],
        compiler_params=pltpu.CompilerParams(collective_id=ident, has_side_effects=True),
    )(cut)
    return out.reshape(n * rows, width)


def reduce_kernel(n, part_ref, out_ref, land, s1, r1, s2, r2):
    me, col = lax.axis_index("samp"), lax.axis_index("par")
    slab = land.shape[-1]
    at = [lax.rem(me + k, n) for k in range(n)]
    back = [lax.rem(me + n - k, n) for k in range(n)]
    peer = [(at[k], col) for k in range(n)]
    cols = lambda j: pl.ds(pl.multiple_of(j * slab, slab), slab)
    greet(peer[1:])
    scatter = [
        remote(part_ref.at[:, cols(at[k])], land.at[k], s1.at[k], r1.at[k], peer[k]) for k in range(1, n)
    ]
    for copy in scatter:
        copy.start()
    total = part_ref[:, cols(me)].astype(jnp.float32)
    for k in range(1, n):
        scatter[k - 1].wait_recv()
        total = total + land[k].astype(jnp.float32)
    out_ref[:, cols(me)] = total.astype(out_ref.dtype)
    spread = [
        remote(out_ref.at[:, cols(me)], out_ref.at[:, cols(me)], s2.at[k], r2.at[k], peer[k])
        for k in range(1, n)
    ]
    for copy in spread:
        copy.start()
    for k in range(1, n):
        remote(out_ref.at[:, cols(me)], out_ref.at[:, cols(back[k])], s2.at[k], r2.at[k], peer[k]).wait_recv()
    for copy in scatter + spread:
        copy.wait_send()


def reduce_all(part, n, ident):
    count, width = part.shape
    vmem = pl.BlockSpec(memory_space=pltpu.VMEM)
    return pl.pallas_call(
        functools.partial(reduce_kernel, n),
        out_shape=jax.ShapeDtypeStruct(part.shape, part.dtype),
        in_specs=[vmem],
        out_specs=vmem,
        scratch_shapes=[pltpu.VMEM((n, count, width // n), part.dtype)]
        + [pltpu.SemaphoreType.DMA((n,)) for _ in range(4)],
        compiler_params=pltpu.CompilerParams(collective_id=ident, has_side_effects=True),
    )(part)


def tiny_kernel(p, part_ref, out_ref, land, s1, r1):
    me, col = lax.axis_index("samp"), lax.axis_index("par")
    at = [lax.rem(col + k, p) for k in range(p)]
    back = [lax.rem(col + p - k, p) for k in range(p)]
    greet([(me, at[k]) for k in range(1, p)])
    copies = [remote(part_ref, land.at[col], s1.at[k], r1.at[k], (me, at[k])) for k in range(1, p)]
    for copy in copies:
        copy.start()
    land[col] = part_ref[...]
    for k in range(1, p):
        remote(part_ref, land.at[back[k]], s1.at[k], r1.at[k], (me, at[k])).wait_recv()
    for copy in copies:
        copy.wait_send()
    total = land[0]
    for j in range(1, p):
        total = total + land[j]
    out_ref[...] = total


def tiny_sum(part, p, ident):
    vmem = pl.BlockSpec(memory_space=pltpu.VMEM)
    return pl.pallas_call(
        functools.partial(tiny_kernel, p),
        out_shape=jax.ShapeDtypeStruct(part.shape, part.dtype),
        in_specs=[vmem],
        out_specs=vmem,
        scratch_shapes=[pltpu.VMEM((p,) + part.shape, part.dtype)]
        + [pltpu.SemaphoreType.DMA((p,)) for _ in range(2)],
        compiler_params=pltpu.CompilerParams(collective_id=ident, has_side_effects=True),
    )(part)


def body(log_derivs, energies, nys_rows):
    rows, width = log_derivs.shape
    n, p = lax.axis_size("samp"), lax.axis_size("par")
    count, rank = energies.shape[1], nys_rows.shape[1]
    scale = 1.0 / math.sqrt(width * p)
    picks = (nys_rows.reshape(rank, 1) == lax.broadcasted_iota(jnp.int32, (rank, rows), 1)).astype(jnp.bfloat16)
    probe = jnp.concatenate([picks, jnp.ones((8, rows), jnp.bfloat16)], axis=0)
    taken = jnp.dot(probe, log_derivs, preferred_element_type=jnp.float32)
    chosen = taken[:rank].astype(jnp.bfloat16)
    sums = taken[rank].reshape(n, 1, width // n)
    aux = jnp.concatenate([energies, picks.astype(jnp.float32).T], axis=1)
    mean, aux_all, chosen_all = gather_rows(sums, aux, chosen, n, n * rows, 0)
    mean = mean.reshape(1, width)
    centered = ((log_derivs.astype(jnp.float32) - mean) * scale).astype(jnp.bfloat16)
    chosen_all = chosen_all.reshape(n * rank, width)
    chosen_all = ((chosen_all.astype(jnp.float32) - mean) * scale).astype(jnp.bfloat16)
    sketch_part = jnp.einsum("rc,kc->rk", centered, chosen_all, preferred_element_type=jnp.float32)
    sketch = sum_and_spread(sketch_part, n, p, 1)
    all_energies = aux_all[:, :, :count].reshape(n * rows, count)
    core_block = jnp.einsum(
        "grj,grk->gjk", aux_all[:, :, count:], sketch.reshape(n, rows, n * rank), precision=lax.Precision.HIGHEST
    ).reshape(n * rank, n * rank)
    factor = jnp.linalg.cholesky(damping * core_block + hdot(sketch.T, sketch))

    def precondition(residual):
        coeffs = factor_solve(factor, hdot(sketch.T, residual))
        result = (residual - hdot(sketch, coeffs)) / damping
        return (result, hdot(result.T, residual))

    start = lax.axis_index("samp") * rows
    solution = jnp.zeros(all_energies.shape, jnp.float32)
    update = 0.0
    residual = all_energies
    precond_res, inner_prev = precondition(residual)
    direction = precond_res
    for iteration in range(ITERS):
        rounded = lax.dynamic_slice_in_dim(direction, start, rows, 0).astype(jnp.bfloat16)
        part = jnp.einsum("rv,rc->vc", rounded, centered, preferred_element_type=jnp.float32)
        projected = reduce_all(part.astype(jnp.bfloat16), n, 2 + 2 * iteration)
        if iteration + 1 < ITERS:
            image_part = jnp.einsum("rc,vc->rv", centered, projected, preferred_element_type=jnp.float32)
            image_k = sum_and_spread(image_part, n, p, 3 + 2 * iteration) + damping * direction
            curvature = hdot(direction.T, image_k)
        else:
            square = jnp.einsum("uc,vc->uv", projected, projected, preferred_element_type=jnp.float32)
            curvature = tiny_sum(square, p, 3 + 2 * iteration) + damping * hdot(direction.T, direction)
        alpha_k = small_solve(curvature, inner_prev)
        solution = solution + hdot(direction, alpha_k)
        update = update + hdot(alpha_k.T, projected.astype(jnp.float32))
        if iteration + 1 < ITERS:
            residual = residual - hdot(image_k, alpha_k)
            precond_res, inner_next = precondition(residual)
            beta_k = small_solve(inner_prev, inner_next)
            direction = precond_res + hdot(direction, beta_k)
            inner_prev = inner_next
    return (update.T, lax.dynamic_slice_in_dim(solution, start, rows, 0))


def solution(mesh):
    return jax.shard_map(
        body,
        mesh=mesh,
        in_specs=(P("samp", "par"), P("samp", None), P("samp", None)),
        out_specs=(P("par", None), P("samp", None)),
        check_vma=False,
    )
```

time: 352 us -> 247 us (0.70)
  Pallas kernels: 0 us -> 164 us
  waiting for transfers between devices: 145 us -> 0 us
  blocking collectives: 106 us -> 0 us
  matrix products: 23.4 us -> 48.5 us
  other arithmetic: 46.2 us -> 30.3 us
  between operations: 14.2 us -> 0.84 us
  local copies, waits for them, and re-layouts: 11.8 us -> 2.62 us
  starting transfers between devices: 5.59 us -> 0 us
    pallas_call x0 -> x6, Pallas kernels: none -> 164 us  [the longest x1 66.6 us: gather_rows(): pl.pallas_call(functools.partial(gather_kernel, n, total_rows), out_shape...]
    psum x1 -> x0, waiting for transfers between devices: 123 us -> none  [gram_body(): lax.psum(jnp.einsum('rc,kc->rk', centered, centered, preferred_element_ty...]
    all_gather x2 -> x0, blocking collectives: 106 us -> none  [the longest x1 97.4 us: gram_body(): all_picks = lax.all_gather(nys_rows, 'samp', axis=0, tiled=True)]
    all_gather x1 -> x0, waiting for transfers between devices: 21.8 us -> none  [gram_body(): lax.all_gather(local_update.astype(jnp.bfloat16), 'samp', axis=0, tiled=T...]
    dot_general x2 -> x7, matrix products: 16.5 us -> 35.6 us  [the longest x2 11.3 us: body(): jnp.einsum('rv,rc->vc', rounded, centered, preferred_element_type=jnp.flo...]
    another operation x4 -> x3, other arithmetic: 15.4 us -> 6.52 us  [body(): factor = jnp.linalg.cholesky(damping * core_block + hdot(sketch.T, sketch))]
    all_to_all x1 -> x0, local copies, waits for them, and re-layouts: 7.59 us -> none  [gram_body(): lax.all_to_all(log_derivs, 'samp', split_axis=1, concat_axis=0, tiled=True)]
    dot_general x15, matrix products: 5.24 us -> 11.3 us  [hdot(): return jnp.dot(left, right, precision=lax.Precision.HIGHEST)]
  transfers between devices with their start and end apart: 3 -> 0, of which waited for: 2 -> 0; matrix products, arithmetic and copies ran while one was open for 3% -> 0% of each run, Pallas kernels for 0% -> 0%
where the time goes in v1:
time: 247 us; the launch traced here: 246 us
  Pallas kernels  164 us (66%)
  matrix products  48.5 us (20%)
  other arithmetic  30.3 us (12%)
  local copies, waits for them, and re-layouts  2.62 us (1%)
    pallas_call x1, Pallas kernels, gather_rows(): pl.pallas_call(functools.partial(gather_kernel, n, total_rows), out_shape...  66.6 us
    pallas_call x2, Pallas kernels, reduce_all(): pl.pallas_call(functools.partial(reduce_kernel, n), out_shape=jax.ShapeDt...  56 us
    pallas_call x2, Pallas kernels, sum_and_spread(): pl.pallas_call(functools.partial(spread_kernel, n, p), out_shape=jax.Shap...  34.8 us
    dot_general x2, matrix products, body(): jnp.einsum('rv,rc->vc', rounded, centered, preferred_element_type=jnp.flo...  11.3 us
    dot_general x15, matrix products, hdot(): return jnp.dot(left, right, precision=lax.Precision.HIGHEST)  11.3 us
    another operation x8, other arithmetic, factor_solve(): lax.linalg.triangular_solve(factor, middle, left_side=True, lower=True, t...  9.37 us
    dot_general x1, matrix products, body(): jnp.einsum('rc,kc->rk', centered, chosen_all, preferred_element_type=jnp....  8.69 us
    convert_element_type x1, other arithmetic, body(): ((log_derivs.astype(jnp.float32) - mean) * scale).astype(jnp.bfloat16)  8.63 us

profile of v1, /device:TPU:0, one launch (start us, length us, event | category | flops | bytes accessed | tf_op | source)
XLA Modules:
  0.0 246.4 jit_solution(6610866937784623076)
XLA Ops:
  0.6 0.8 iota_compare_fusion.5
  1.4 4.6 %fusion.20 = f32[16,65536]{1,0:T(8,128)S(1)} fusion(bf16[64,65536]{1,0:T(8,128)(2,1)} %param.12, pred[8,64]{1,0:T(8,128)(4,1)S(1)} %iota_compare_fusion.5), kind=kOutput, calls=%fused_computation.39 | convolution fusion | flops 134217728 | bytes 12583424 | tf_op jit(solution)/shard_map/dot_general | solution.py:268
  6.4 66.6 %shard_map.50 = (f32[8,1,8192]{2,1,0:T(1,128)S(1)}, f32[8,64,16]{2,1,0:T(8,128)S(1)}, bf16[8,8,65536]{2,1,0:T(8,128)(2,1)}) custom-call(f32[8,1,8192]{2,1,0:T(1,128)S(1)} %bitcast.135, f32[64,16]{1,0:T(8,128)S(1)} %copy.49.aux_ref, bf16[8,65536]{1,0:T(8,128)(2,1)S(1)} %slice.40.chosen_ref), custom_call_target="tpu_custom_call" | custom-call | tf_op jit(solution)/shard_map/pallas_call | solution.py:99
  73.0 8.6 %multiply_convert_fusion.1 = bf16[64,65536]{1,0:T(8,128)(2,1)} fusion(bf16[64,65536]{1,0:T(8,128)(2,1)} %param.12, f32[65536]{0:T(1024)S(1)} %bitcast.136), kind=kLoop, calls=%fused_computation.4 | loop fusion | flops 16777216 | bytes 17039360 | tf_op jit(solution)/shard_map/convert_element_type | solution.py:274
  81.7 8.7 %fusion.1.part_ref = f32[4,16,64]{2,1,0:T(8,128)} fusion(bf16[4,16,65536]{2,1,0:T(8,128)(2,1)} %bitcast.138, bf16[8,8,65536]{2,1,0:T(8,128)(2,1)} %get-tuple-element.12, f32[65536]{0:T(1024)S(1)} %bitcast.137), kind=kOutput, calls=%fused_computation.6 | convolution fusion | flops 553648128 | bytes 17055744 | tf_op jit(solution)/shard_map/rc,kc->rk/dot_general | solution.py:277
  90.4 18.0 %shard_map.51 = f32[32,16,64]{2,1,0:T(8,128)} custom-call(f32[4,16,64]{2,1,0:T(8,128)} %fusion.1.part_ref), custom_call_target="tpu_custom_call" | custom-call | tf_op jit(solution)/shard_map/pallas_call | solution.py:167
  108.4 1.6 fusion.6
  110.0 1.6 fusion.5
  111.8 5.8 %cholesky.34 = f32[64,64]{1,0:T(8,128)S(1)} custom-call(f32[64,64]{1,0:T(8,128)S(1)} %fusion.19), custom_call_target="Cholesky" | custom-call | tf_op jit(solution)/shard_map/jit(cholesky)/cholesky | solution.py:283
  119.0 4.9 %custom-call.24 = f32[1,64,64]{1,2,0:T(8,128)S(1)} custom-call(f32[1,64,64]{2,1,0:T(8,128)S(1)} %fusion.10), custom_call_target="InvertDiagBlocksLowerTriangular" | custom-call | tf_op jit(solution)/shard_map/triangular_solve/custom-call.3 | solution.py:21
  123.9 1.5 fusion.49
  125.8 1.3 broadcast_multiply_fusion
  127.1 5.6 %convolution_convert_fusion.1.part_ref = bf16[8,65536]{1,0:T(8,128)(2,1)} fusion(bf16[64,65536]{1,0:T(8,128)(2,1)} %multiply_convert_fusion.1, bf16[512,8]{0,1:T(8,128)(2,1)S(1)} %get-tuple-element.13, s32[]{:T(128)S(6)} %select_n.13), kind=kOutput, calls=%fused_computation.2 | convolution fusion | flops 67633152 | bytes 9439236 | tf_op jit(solution)/shard_map/rv,rc->vc/dot_general | solution.py:298
  132.7 27.7 %shard_map.52 = bf16[8,65536]{1,0:T(8,128)(2,1)} custom-call(bf16[8,65536]{1,0:T(8,128)(2,1)} %convolution_convert_fusion.1.part_ref), custom_call_target="tpu_custom_call" | custom-call | tf_op jit(solution)/shard_map/pallas_call | solution.py:218
  160.5 6.5 %fusion.50 = f32[64,8]{1,0:T(8,128)} fusion(bf16[64,65536]{1,0:T(8,128)(2,1)} %multiply_convert_fusion.1, bf16[8,65536]{1,0:T(8,128)(2,1)} %shard_map.52), kind=kOutput, calls=%fused_computation.89 | convolution fusion | flops 67108864 | bytes 9439232 | tf_op jit(solution)/shard_map/rc,vc->rv/dot_general | solution.py:301
  167.0 16.8 %shard_map.53 = f32[32,16,8]{2,1,0:T(8,128)} custom-call(f32[4,16,8]{2,1,0:T(8,128)} %bitcast.145), custom_call_target="tpu_custom_call" | custom-call | tf_op jit(solution)/shard_map/pallas_call | solution.py:167
  183.8 1.0 copy.56
  193.2 5.6 %convolution_convert_fusion.part_ref = bf16[8,65536]{1,0:T(8,128)(2,1)} fusion(bf16[64,65536]{1,0:T(8,128)(2,1)} %multiply_convert_fusion.1, f32[512,8]{0,1:T(8,128)S(1)} %convolution_add_fusion.1, s32[]{:T(128)S(6)} %select_n.13), kind=kOutput, calls=%fused_computation.1 | convolution fusion | flops 67633152 | bytes 9439236 | tf_op jit(solution)/shard_map/rv,rc->vc/dot_general | solution.py:298
  198.8 28.2 %shard_map.54 = bf16[8,65536]{1,0:T(8,128)(2,1)} custom-call(bf16[8,65536]{1,0:T(8,128)(2,1)} %convolution_convert_fusion.part_ref), custom_call_target="tpu_custom_call" | custom-call | tf_op jit(solution)/shard_map/pallas_call | solution.py:218
  227.1 2.9 %fusion.54.part_ref = f32[8,8]{1,0:T(8,128)} fusion(bf16[8,65536]{1,0:T(8,128)(2,1)} %shard_map.54), kind=kOutput, calls=%fused_computation.93 | convolution fusion | flops 8388608 | bytes 1048832 | tf_op jit(solution)/shard_map/uc,vc->uv/dot_general | solution.py:305
  230.0 6.8 %shard_map.55 = f32[8,8]{1,0:T(8,128)} custom-call(f32[8,8]{1,0:T(8,128)} %fusion.54.part_ref), custom_call_target="tpu_custom_call" | custom-call | tf_op jit(solution)/shard_map/pallas_call | solution.py:250
  236.8 0.7 copy.65
  241.6 1.0 fusion.51
  242.7 3.7 %convolution_add_fusion = f32[65536,8]{0,1:T(8,128)} fusion(f32[65536,8]{0,1:T(8,128)S(1)} %fusion.51, bf16[8,65536]{1,0:T(8,128)(2,1)} %shard_map.54, f32[8,8]{1,0:T(8,128)S(1)} %fusion.27), kind=kOutput, calls=%fused_computation | convolution fusion | flops 50855936 | bytes 5243136 | tf_op jit(solution)/shard_map/dot_general | solution.py:29
  (63 shorter events, 14.7 us)
Async XLA Ops:
  0.6 5.6 %copy-start.3 = (s32[1,8]{1,0:T(1,128)S(1)}, s32[1,8]{1,0:T(1,128)}, u32[]{:S(2)}) copy-start(s32[1,8]{1,0:T(1,128)} %param.14) | copy-start | bytes 100
  0.6 5.7 %copy-start.2 = (f32[64,8]{0,1:T(8,128)S(1)}, f32[64,8]{0,1:T(8,128)}, u32[]{:S(2)}) copy-start(f32[64,8]{0,1:T(8,128)} %param.13) | copy-start | bytes 6148
  132.7 58.8 %copy-start = (f32[32,16,64]{2,1,0:T(8,128)S(1)}, f32[32,16,64]{2,1,0:T(8,128)}, u32[]{:S(2)}) copy-start(f32[32,16,64]{2,1,0:T(8,128)} %shard_map.51) | copy-start | bytes 393220
  167.0 74.6 %copy-start.1 = (bf16[8,65536]{1,0:T(8,128)(2,1)S(1)}, bf16[8,65536]{1,0:T(8,128)(2,1)}, u32[]{:S(2)}) copy-start(bf16[8,65536]{1,0:T(8,128)(2,1)} %shard_map.52) | copy-start | bytes 3145732

commit v2 on v1

v2 whole, which is shorter than its diff:
```python
import functools
import math

import jax
import jax.numpy as jnp
from jax import lax
from jax.experimental import pallas as pl
from jax.experimental.pallas import tpu as pltpu
from jax.sharding import PartitionSpec as P

ITERS = 2


damping = 0.5

MESH = pl.DeviceIdType.MESH


def factor_solve(factor, right):
    middle = lax.linalg.triangular_solve(factor, right, left_side=True, lower=True)
    return lax.linalg.triangular_solve(factor, middle, left_side=True, lower=True, transpose_a=True)


def eliminate_kernel(matrix_ref, right_ref, out_ref):
    left, right = matrix_ref[...], right_ref[...]
    row = lax.broadcasted_iota(jnp.int32, left.shape, 0)
    for i in range(left.shape[0]):
        column = left[:, i:i + 1]
        pivot = left[i:i + 1, i:i + 1]
        left_row = left[i:i + 1, :] / pivot
        right_row = right[i:i + 1, :] / pivot
        left = jnp.where(row == i, left_row, left - column * left_row)
        right = jnp.where(row == i, right_row, right - column * right_row)
    out_ref[...] = right


def small_solve(matrix, right):
    matrix = 0.5 * (matrix + matrix.T)
    return pl.pallas_call(
        eliminate_kernel, out_shape=jax.ShapeDtypeStruct(right.shape, right.dtype)
    )(matrix, right)


def hdot(left, right):
    return jnp.dot(left, right, precision=lax.Precision.HIGHEST)


def greet(peers):
    barrier = pltpu.get_barrier_semaphore()
    for peer in peers:
        pl.semaphore_signal(barrier, inc=1, device_id=peer, device_id_type=MESH)
    pl.semaphore_wait(barrier, len(peers))


def remote(src, dst, send, recv, peer):
    return pltpu.make_async_remote_copy(
        src_ref=src, dst_ref=dst, send_sem=send, recv_sem=recv, device_id=peer, device_id_type=MESH
    )


def gather_kernel(n, total_rows, scale, sums_ref, aux_ref, chosen_ref, full_ref, mean_ref, aux_out, rows_out, centered_ref,
                  land, own, full, s1, r1, s2, r2, s3, r3, s4, r4, s5, r5, s6, r6, local):
    me, col = lax.axis_index("samp"), lax.axis_index("par")
    at = [lax.rem(me + k, n) for k in range(n)]
    back = [lax.rem(me + n - k, n) for k in range(n)]
    peer = [(at[k], col) for k in range(n)]
    pair = (jnp.bitwise_xor(me, 1), col)
    width = chosen_ref.shape[1]
    half = width // 2
    part = [pl.ds(0, half), pl.ds(half, half)]
    load = pltpu.make_async_copy(full_ref, full, local.at[2])
    load.start()
    greet(peer[1:])
    scatter = [remote(sums_ref.at[at[k]], land.at[k], s1.at[k], r1.at[k], peer[k]) for k in range(1, n)]
    for copy in scatter:
        copy.start()
    sent = list(scatter)
    quad = n == 8
    beside = [jnp.bitwise_xor(me, 2), jnp.bitwise_xor(me, 4)]
    if quad:
        first = [
            remote(chosen_ref.at[:, part[d]], rows_out.at[me, :, part[d]], s4.at[d], r4.at[d], (beside[d], col))
            for d in range(2)
        ]
        for copy in first:
            copy.start()
        sent += first
    auxes = [remote(aux_ref, aux_out.at[me], s2.at[k], r2.at[k], peer[k]) for k in range(1, n)]
    mine = pltpu.make_async_copy(aux_ref, aux_out.at[me], local.at[0])
    mine.start()
    keep = pltpu.make_async_copy(chosen_ref, rows_out.at[me], local.at[1])
    keep.start()
    total = sums_ref[me]
    for k in range(1, n):
        scatter[k - 1].wait_recv()
        total = total + land[k]
    own[...] = total / total_rows
    mean_ref[me] = own[...]
    spread = [remote(own, mean_ref.at[me], s3.at[k], r3.at[k], peer[k]) for k in range(1, n)]
    for copy in spread + auxes:
        copy.start()
    sent += spread + auxes
    over = [remote(chosen_ref, rows_out.at[me], s5.at[0], r5.at[0], pair)]
    over[0].start()
    if quad:
        second = [
            remote(chosen_ref.at[:, part[1 - d]], rows_out.at[me, :, part[1 - d]], s4.at[2 + d], r4.at[2 + d],
                   (beside[d], col))
            for d in range(2)
        ]
        for copy in second:
            copy.start()
        sent += second
        for d in range(2):
            view = rows_out.at[beside[d], :, part[d]]
            remote(view, view, s4.at[d], r4.at[d], pair).wait_recv()
            step = remote(view, view, s4.at[4 + d], r4.at[4 + d], (beside[1 - d], col))
            step.start()
            sent.append(step)
    else:
        far = [remote(chosen_ref, rows_out.at[me], s4.at[k], r4.at[k], peer[k]) for k in range(2, n, 2)]
        for copy in far:
            copy.start()
        sent += far
    for k in range(1, n):
        remote(own, mean_ref.at[back[k]], s3.at[k], r3.at[k], peer[k]).wait_recv()
    load.wait()
    slab = width // n
    tile = math.gcd(slab, 1024)

    @pl.loop(0, n)
    def _(j):
        @pl.loop(0, slab // tile)
        def _(t):
            inner = pl.multiple_of(t * tile, tile)
            cols = pl.ds(pl.multiple_of(j * slab + inner, tile), tile)
            mean = mean_ref[j, :, pl.ds(inner, tile)]
            centered_ref[:, cols] = ((full[:, cols].astype(jnp.float32) - mean) * scale).astype(jnp.bfloat16)

    if quad:
        for d in range(2):
            view = rows_out.at[beside[d], :, part[1 - d]]
            remote(view, view, s4.at[2 + d], r4.at[2 + d], pair).wait_recv()
            block = rows_out.at[beside[d]]
            step = remote(block, block, s5.at[1 + d], r5.at[1 + d], pair)
            step.start()
            over.append(step)
        cross = jnp.bitwise_xor(me, 6)
        for d in range(2):
            view = rows_out.at[cross, :, part[d]]
            remote(view, view, s4.at[4 + d], r4.at[4 + d], pair).wait_recv()
            step = remote(view, view, s5.at[3 + d], r5.at[3 + d], pair)
            step.start()
            over.append(step)
        block = rows_out.at[jnp.bitwise_xor(me, 1)]
        remote(block, block, s5.at[0], r5.at[0], pair).wait_recv()
        for d in range(2):
            block = rows_out.at[jnp.bitwise_xor(me, 3 + 2 * d)]
            remote(block, block, s5.at[1 + d], r5.at[1 + d], pair).wait_recv()
            view = rows_out.at[jnp.bitwise_xor(me, 7), :, part[d]]
            remote(view, view, s5.at[3 + d], r5.at[3 + d], pair).wait_recv()
    else:
        for k in range(2, n, 2):
            block = rows_out.at[back[k]]
            remote(block, block, s4.at[k], r4.at[k], pair).wait_recv()
            step = remote(block, block, s5.at[k], r5.at[k], pair)
            step.start()
            over.append(step)
        for k in range(0, n, 2):
            block = rows_out.at[lax.rem(pair[0] + n - k, n)]
            remote(block, block, s5.at[k], r5.at[k], pair).wait_recv()
    for k in range(1, n):
        remote(aux_ref, aux_out.at[back[k]], s2.at[k], r2.at[k], peer[k]).wait_recv()
    for copy in sent + over:
        copy.wait_send()
    mine.wait()
    keep.wait()


def gather_rows(sums, aux, chosen, full, n, total_rows, scale, ident):
    dma = lambda: pltpu.SemaphoreType.DMA((n,))
    vmem = pl.BlockSpec(memory_space=pltpu.VMEM)
    slab = sums.shape[-1]
    return pl.pallas_call(
        functools.partial(gather_kernel, n, total_rows, scale),
        out_shape=(
            jax.ShapeDtypeStruct(sums.shape, jnp.float32),
            jax.ShapeDtypeStruct((n,) + aux.shape, jnp.float32),
            jax.ShapeDtypeStruct((n,) + chosen.shape, chosen.dtype),
            jax.ShapeDtypeStruct(full.shape, full.dtype),
        ),
        in_specs=[vmem, vmem, vmem, pl.BlockSpec(memory_space=pl.ANY)],
        out_specs=(vmem, vmem, vmem, vmem),
        scratch_shapes=[
            pltpu.VMEM(sums.shape, jnp.float32),
            pltpu.VMEM((1, slab), jnp.float32),
            pltpu.VMEM(full.shape, full.dtype),
        ] + [dma() for _ in range(12)] + [pltpu.SemaphoreType.DMA((3,))],
        compiler_params=pltpu.CompilerParams(
            collective_id=ident, has_side_effects=True, vmem_limit_bytes=60 * 2**20
        ),
    )(sums, aux, chosen, full)


def spread_kernel(n, p, part_ref, out_ref, land, own, s1, r1, s2, r2):
    me, col = lax.axis_index("samp"), lax.axis_index("par")
    beside = [lax.rem(col + k, p) for k in range(p)]
    at = [lax.rem(me + k, n) for k in range(n)]
    back = [lax.rem(me + n - k, n) for k in range(n)]
    greet([(me, beside[k]) for k in range(1, p)] + [(at[k], col) for k in range(1, n)])
    sums = [remote(part_ref, land.at[col], s1.at[k], r1.at[k], (me, beside[k])) for k in range(1, p)]
    for copy in sums:
        copy.start()
    land[col] = part_ref[...]
    for k in range(1, p):
        there = lax.rem(col + p - k, p)
        remote(part_ref, land.at[there], s1.at[k], r1.at[k], (me, beside[k])).wait_recv()
    total = land[0]
    for j in range(1, p):
        total = total + land[j]
    own[...] = total
    out_ref[me] = total
    hops = [remote(own, out_ref.at[me], s2.at[k], r2.at[k], (at[k], col)) for k in range(1, n)]
    for copy in hops:
        copy.start()
    for k in range(1, n):
        remote(own, out_ref.at[back[k]], s2.at[k], r2.at[k], (at[k], col)).wait_recv()
    for copy in sums + hops:
        copy.wait_send()


def sum_and_spread(part, n, p, ident):
    vmem = pl.BlockSpec(memory_space=pltpu.VMEM)
    return pl.pallas_call(
        functools.partial(spread_kernel, n, p),
        out_shape=jax.ShapeDtypeStruct((n,) + part.shape, jnp.float32),
        in_specs=[vmem],
        out_specs=vmem,
        scratch_shapes=[
            pltpu.VMEM((p,) + part.shape, jnp.float32),
            pltpu.VMEM(part.shape, jnp.float32),
            pltpu.SemaphoreType.DMA((p,)),
            pltpu.SemaphoreType.DMA((p,)),
            pltpu.SemaphoreType.DMA((n,)),
            pltpu.SemaphoreType.DMA((n,)),
        ],
        compiler_params=pltpu.CompilerParams(collective_id=ident, has_side_effects=True),
    )(part)


def reduce_kernel(n, part_ref, out_ref, land, both, inbox, s0, r0, s1, r1, s2, r2, s3, r3):
    me, col = lax.axis_index("samp"), lax.axis_index("par")
    outer = n // 2
    slab = part_ref.shape[1] // n
    half = slab * outer
    i, o = lax.rem(me, 2), me // 2
    pair = (jnp.bitwise_xor(me, 1), col)
    at = [lax.rem(o + k, outer) for k in range(outer)]
    back = [lax.rem(o + outer - k, outer) for k in range(outer)]
    peer = [(at[k] * 2 + i, col) for k in range(outer)]
    cols = lambda j: pl.ds(pl.multiple_of(j * slab, slab), slab)
    halves = lambda j: pl.ds(pl.multiple_of(j * half, half), half)
    greet([pair] + peer[1:])
    swap = remote(part_ref.at[:, halves(1 - i)], land, s0.at[0], r0.at[0], pair)
    swap.start()
    swap.wait_recv()
    both[...] = (part_ref[:, halves(i)].astype(jnp.float32) + land[...].astype(jnp.float32)).astype(both.dtype)
    scatter = [remote(both.at[:, cols(at[k])], inbox.at[k], s1.at[k], r1.at[k], peer[k]) for k in range(1, outer)]
    for copy in scatter:
        copy.start()
    total = part_ref[:, cols(i * outer + o)].astype(jnp.float32) + land[:, cols(o)].astype(jnp.float32)
    for k in range(1, outer):
        scatter[k - 1].wait_recv()
        total = total + inbox[k].astype(jnp.float32)
    home = cols(i * outer + o)
    out_ref[:, home] = total.astype(out_ref.dtype)
    mine = out_ref.at[:, home]
    spread = [remote(mine, mine, s2.at[k], r2.at[k], peer[k]) for k in range(1, outer)]
    spread.append(remote(mine, mine, s3.at[0], r3.at[0], pair))
    for copy in spread:
        copy.start()
    for k in range(1, outer):
        block = out_ref.at[:, cols(i * outer + back[k])]
        remote(block, block, s2.at[k], r2.at[k], pair).wait_recv()
        step = remote(block, block, s3.at[k], r3.at[k], pair)
        step.start()
        spread.append(step)
    for k in range(outer):
        block = out_ref.at[:, cols((1 - i) * outer + back[k])]
        remote(block, block, s3.at[k], r3.at[k], pair).wait_recv()
    for copy in [swap] + scatter + spread:
        copy.wait_send()


def reduce_all(part, n, ident):
    count, width = part.shape
    outer = n // 2
    vmem = pl.BlockSpec(memory_space=pltpu.VMEM)
    return pl.pallas_call(
        functools.partial(reduce_kernel, n),
        out_shape=jax.ShapeDtypeStruct(part.shape, part.dtype),
        in_specs=[vmem],
        out_specs=vmem,
        scratch_shapes=[
            pltpu.VMEM((count, width // 2), part.dtype),
            pltpu.VMEM((count, width // 2), part.dtype),
            pltpu.VMEM((outer, count, width // n), part.dtype),
        ]
        + [pltpu.SemaphoreType.DMA((outer,)) for _ in range(8)],
        compiler_params=pltpu.CompilerParams(collective_id=ident, has_side_effects=True),
    )(part)


def tiny_kernel(p, part_ref, out_ref, land, s1, r1):
    me, col = lax.axis_index("samp"), lax.axis_index("par")
    at = [lax.rem(col + k, p) for k in range(p)]
    back = [lax.rem(col + p - k, p) for k in range(p)]
    greet([(me, at[k]) for k in range(1, p)])
    copies = [remote(part_ref, land.at[col], s1.at[k], r1.at[k], (me, at[k])) for k in range(1, p)]
    for copy in copies:
        copy.start()
    land[col] = part_ref[...]
    for k in range(1, p):
        remote(part_ref, land.at[back[k]], s1.at[k], r1.at[k], (me, at[k])).wait_recv()
    for copy in copies:
        copy.wait_send()
    total = land[0]
    for j in range(1, p):
        total = total + land[j]
    out_ref[...] = total


def tiny_sum(part, p, ident):
    vmem = pl.BlockSpec(memory_space=pltpu.VMEM)
    return pl.pallas_call(
        functools.partial(tiny_kernel, p),
        out_shape=jax.ShapeDtypeStruct(part.shape, part.dtype),
        in_specs=[vmem],
        out_specs=vmem,
        scratch_shapes=[pltpu.VMEM((p,) + part.shape, part.dtype)]
        + [pltpu.SemaphoreType.DMA((p,)) for _ in range(2)],
        compiler_params=pltpu.CompilerParams(collective_id=ident, has_side_effects=True),
    )(part)


def body(log_derivs, energies, nys_rows):
    rows, width = log_derivs.shape
    n, p = lax.axis_size("samp"), lax.axis_size("par")
    count, rank = energies.shape[1], nys_rows.shape[1]
    scale = 1.0 / math.sqrt(width * p)
    picks = (nys_rows.reshape(rank, 1) == lax.broadcasted_iota(jnp.int32, (rank, rows), 1)).astype(jnp.bfloat16)
    probe = jnp.concatenate([picks, jnp.ones((8, rows), jnp.bfloat16)], axis=0)
    taken = jnp.dot(probe, log_derivs, preferred_element_type=jnp.float32)
    chosen = taken[:rank].astype(jnp.bfloat16)
    sums = taken[rank].reshape(n, 1, width // n)
    aux = jnp.concatenate([energies, picks.astype(jnp.float32).T], axis=1)
    mean, aux_all, chosen_all, centered = gather_rows(sums, aux, chosen, log_derivs, n, n * rows, scale, 0)
    mean = mean.reshape(1, width)
    chosen_all = chosen_all.reshape(n * rank, width)
    chosen_all = ((chosen_all.astype(jnp.float32) - mean) * scale).astype(jnp.bfloat16)
    sketch_part = jnp.einsum("rc,kc->rk", centered, chosen_all, preferred_element_type=jnp.float32)
    sketch = sum_and_spread(sketch_part, n, p, 1).reshape(n * rows, n * rank)
    all_energies = aux_all[:, :, :count].reshape(n * rows, count)
    core_block = jnp.einsum(
        "grj,grk->gjk", aux_all[:, :, count:], sketch.reshape(n, rows, n * rank), precision=lax.Precision.HIGHEST
    ).reshape(n * rank, n * rank)
    factor = jnp.linalg.cholesky(damping * core_block + hdot(sketch.T, sketch))

    def precondition(residual):
        coeffs = factor_solve(factor, hdot(sketch.T, residual))
        result = (residual - hdot(sketch, coeffs)) / damping
        return (result, hdot(result.T, residual))

    start = lax.axis_index("samp") * rows
    solution = jnp.zeros(all_energies.shape, jnp.float32)
    update = 0.0
    residual = all_energies
    precond_res, inner_prev = precondition(residual)
    direction = precond_res
    for iteration in range(ITERS):
        rounded = lax.dynamic_slice_in_dim(direction, start, rows, 0).astype(jnp.bfloat16)
        part = jnp.einsum("rv,rc->vc", rounded, centered, preferred_element_type=jnp.float32)
        projected = reduce_all(part.astype(jnp.bfloat16), n, 2 + 2 * iteration)
        if iteration + 1 < ITERS:
            image_part = jnp.einsum("rc,vc->vr", centered, projected, preferred_element_type=jnp.float32)
            image_k = sum_and_spread(image_part, n, p, 3 + 2 * iteration)
            image_k = image_k.transpose(0, 2, 1).reshape(n * rows, count) + damping * direction
            curvature = hdot(direction.T, image_k)
        else:
            square = jnp.einsum("uc,vc->uv", projected, projected, preferred_element_type=jnp.float32)
            curvature = tiny_sum(square, p, 3 + 2 * iteration) + damping * hdot(direction.T, direction)
        alpha_k = small_solve(curvature, inner_prev)
        solution = solution + hdot(direction, alpha_k)
        update = update + hdot(alpha_k.T, projected.astype(jnp.float32))
        if iteration + 1 < ITERS:
            residual = residual - hdot(image_k, alpha_k)
            precond_res, inner_next = precondition(residual)
            beta_k = small_solve(inner_prev, inner_next)
            direction = precond_res + hdot(direction, beta_k)
            inner_prev = inner_next
    return (update.T, lax.dynamic_slice_in_dim(solution, start, rows, 0))


def solution(mesh):
    return jax.shard_map(
        body,
        mesh=mesh,
        in_specs=(P("samp", "par"), P("samp", None), P("samp", None)),
        out_specs=(P("par", None), P("samp", None)),
        check_vma=False,
    )
```

time: 247 us -> 213 us (0.86)
  Pallas kernels: 164 us -> 140 us
  other arithmetic: 30.3 us -> 15.5 us
  matrix products: 48.5 us -> 52.3 us
    pallas_call x2, Pallas kernels: 34.8 us -> 23.7 us  [sum_and_spread(): pl.pallas_call(functools.partial(spread_kernel, n, p), out_shape=jax.Shap...]
    pallas_call x2, Pallas kernels: 56 us -> 45.6 us  [reduce_all(): pl.pallas_call(functools.partial(reduce_kernel, n), out_shape=jax.ShapeDt...]
    convert_element_type x1 -> x0, other arithmetic: 8.63 us -> none  [body(): ((log_derivs.astype(jnp.float32) - mean) * scale).astype(jnp.bfloat16)]
    dot_general x15, matrix products: 11.3 us -> 15.9 us  [hdot(): return jnp.dot(left, right, precision=lax.Precision.HIGHEST)]
    another operation x9 -> x0, other arithmetic: 4.23 us -> none  [small_solve(): return factor_solve(jnp.linalg.cholesky(matrix), right)]
    another operation x8 -> x2, other arithmetic: 9.37 us -> 5.55 us  [factor_solve(): lax.linalg.triangular_solve(factor, middle, left_side=True, lower=True, t...]
    pallas_call x1 -> x4, Pallas kernels: 66.6 us -> 63.7 us  [the longest x1 57.9 us: gather_rows(): pl.pallas_call(functools.partial(gather_kernel, n, total_rows, scale), ou...]
where the time goes in v2:
time: 213 us; the launch traced here: 212 us
  Pallas kernels  140 us (66%)
  matrix products  52.3 us (25%)
  other arithmetic  15.5 us (7%)
  local copies, waits for them, and re-layouts  3.95 us (2%)
    pallas_call x1, Pallas kernels, gather_rows(): pl.pallas_call(functools.partial(gather_kernel, n, total_rows, scale), ou...  57.9 us
    pallas_call x2, Pallas kernels, reduce_all(): pl.pallas_call(functools.partial(reduce_kernel, n), out_shape=jax.ShapeDt...  45.6 us
    pallas_call x2, Pallas kernels, sum_and_spread(): pl.pallas_call(functools.partial(spread_kernel, n, p), out_shape=jax.Shap...  23.7 us
    dot_general x15, matrix products, hdot(): return jnp.dot(left, right, precision=lax.Precision.HIGHEST)  15.9 us
    dot_general x2, matrix products, body(): jnp.einsum('rv,rc->vc', rounded, centered, preferred_element_type=jnp.flo...  11.3 us
    dot_general x1, matrix products, body(): jnp.einsum('rc,kc->rk', centered, chosen_all, preferred_element_type=jnp....  8.75 us
    pallas_call x1, Pallas kernels, tiny_sum(): pl.pallas_call(functools.partial(tiny_kernel, p), out_shape=jax.ShapeDtyp...  6.77 us
    dot_general x1, matrix products, body(): jnp.einsum('rc,vc->vr', centered, projected, preferred_element_type=jnp.f...  6.59 us

profile of v2, /device:TPU:0, one launch (start us, length us, event | category | flops | bytes accessed | tf_op | source)
XLA Modules:
  0.0 212.2 jit_solution(13456809447783695111)
XLA Ops:
  1.4 4.6 %fusion.22 = f32[16,65536]{1,0:T(8,128)S(1)} fusion(bf16[64,65536]{1,0:T(8,128)(2,1)} %full_ref.1, pred[8,64]{1,0:T(8,128)(4,1)S(1)} %iota_compare_fusion.3), kind=kOutput, calls=%fused_computation.41 | convolution fusion | flops 134217728 | bytes 12583424 | tf_op jit(solution)/shard_map/dot_general | solution.py:353
  6.0 1.1 slice.34.chosen_ref
  8.7 57.9 %shard_map.50 = (f32[8,1,8192]{2,1,0:T(1,128)}, f32[8,64,16]{2,1,0:T(8,128)}, bf16[8,8,65536]{2,1,0:T(8,128)(2,1)}, bf16[64,65536]{1,0:T(8,128)(2,1)}) custom-call(f32[8,1,8192]{2,1,0:T(1,128)} %bitcast.99, f32[64,16]{1,0:T(8,128)} %copy.28.aux_ref, bf16[8,65536]{1,0:T(8,128)(2,1)} %slice.34.chosen_ref, bf16[64,65536]{1,0:T(8,128)(2,1)} %full_ref.1), custom_call_target="tpu_custom_call" | custom-call | tf_op jit(solution)/shard_map/pallas_call | solution.py:184
  66.6 8.7 %fusion.2.part_ref = f32[64,64]{1,0:T(8,128)} fusion(bf16[64,65536]{1,0:T(8,128)(2,1)} %get-tuple-element.9, bf16[8,8,65536]{2,1,0:T(8,128)(2,1)} %get-tuple-element.10, f32[65536]{0:T(1024)} %bitcast.103), kind=kOutput, calls=%fused_computation.6 | convolution fusion | flops 553648128 | bytes 17055744 | tf_op jit(solution)/shard_map/rc,kc->rk/dot_general | solution.py:361
  75.4 13.3 %shard_map.51 = f32[8,64,64]{2,1,0:T(8,128)} custom-call(f32[64,64]{1,0:T(8,128)} %fusion.2.part_ref), custom_call_target="tpu_custom_call" | custom-call | tf_op jit(solution)/shard_map/pallas_call | solution.py:234
  88.7 1.6 fusion.8
  90.4 1.6 fusion.7
  92.1 5.8 %cholesky.18 = f32[64,64]{1,0:T(8,128)S(1)} custom-call(f32[64,64]{1,0:T(8,128)S(1)} %fusion.21), custom_call_target="Cholesky" | custom-call | tf_op jit(solution)/shard_map/jit(cholesky)/cholesky | solution.py:367
  99.3 4.9 %custom-call.12 = f32[1,64,64]{1,2,0:T(8,128)S(1)} custom-call(f32[1,64,64]{2,1,0:T(8,128)S(1)} %fusion.12), custom_call_target="InvertDiagBlocksLowerTriangular" | custom-call | tf_op jit(solution)/shard_map/triangular_solve/custom-call.2 | solution.py:21
  104.2 1.5 convolution_bitcast_fusion.1
  106.1 1.3 broadcast_multiply_fusion
  108.3 5.7 %convolution_convert_fusion.1.part_ref = bf16[8,65536]{1,0:T(8,128)(2,1)} fusion(bf16[64,65536]{1,0:T(8,128)(2,1)} %get-tuple-element.9, bf16[512,8]{0,1:T(8,128)(2,1)S(1)} %get-tuple-element.12, s32[]{:T(128)S(6)} %select_n.10), kind=kOutput, calls=%fused_computation.2 | convolution fusion | flops 67633152 | bytes 9439236 | tf_op jit(solution)/shard_map/rv,rc->vc/dot_general | solution.py:382
  113.9 23.3 %shard_map.52 = bf16[8,65536]{1,0:T(8,128)(2,1)} custom-call(bf16[8,65536]{1,0:T(8,128)(2,1)} %convolution_convert_fusion.1.part_ref), custom_call_target="tpu_custom_call" | custom-call | tf_op jit(solution)/shard_map/pallas_call | solution.py:299
  137.3 6.6 %fusion.37.part_ref = f32[8,64]{1,0:T(8,128)} fusion(bf16[8,65536]{1,0:T(8,128)(2,1)} %shard_map.52, bf16[64,65536]{1,0:T(8,128)(2,1)} %get-tuple-element.9), kind=kOutput, calls=%fused_computation.65 | convolution fusion | flops 67108864 | bytes 9439232 | tf_op jit(solution)/shard_map/rc,vc->vr/dot_general | solution.py:385
  143.9 10.4 %shard_map.53 = f32[8,8,64]{2,1,0:T(8,128)} custom-call(f32[8,64]{1,0:T(8,128)} %fusion.37.part_ref), custom_call_target="tpu_custom_call" | custom-call | tf_op jit(solution)/shard_map/pallas_call | solution.py:234
  156.0 1.9 shard_map.54
  162.1 1.9 shard_map.55
  164.9 5.6 %convolution_convert_fusion.part_ref = bf16[8,65536]{1,0:T(8,128)(2,1)} fusion(bf16[64,65536]{1,0:T(8,128)(2,1)} %get-tuple-element.9, f32[512,8]{0,1:T(8,128)S(1)} %convolution_add_fusion.1, s32[]{:T(128)S(6)} %select_n.10), kind=kOutput, calls=%fused_computation.1 | convolution fusion | flops 67633152 | bytes 9439236 | tf_op jit(solution)/shard_map/rv,rc->vc/dot_general | solution.py:382
  170.5 22.3 %shard_map.56 = bf16[8,65536]{1,0:T(8,128)(2,1)} custom-call(bf16[8,65536]{1,0:T(8,128)(2,1)} %convolution_convert_fusion.part_ref), custom_call_target="tpu_custom_call" | custom-call | tf_op jit(solution)/shard_map/pallas_call | solution.py:299
  192.8 2.9 %fusion.41.part_ref = f32[8,8]{1,0:T(8,128)} fusion(bf16[8,65536]{1,0:T(8,128)(2,1)} %shard_map.56), kind=kOutput, calls=%fused_computation.69 | convolution fusion | flops 8388608 | bytes 1048832 | tf_op jit(solution)/shard_map/uc,vc->uv/dot_general | solution.py:390
  195.7 6.8 %shard_map.57 = f32[8,8]{1,0:T(8,128)} custom-call(f32[8,8]{1,0:T(8,128)} %fusion.41.part_ref), custom_call_target="tpu_custom_call" | custom-call | tf_op jit(solution)/shard_map/pallas_call | solution.py:335
  204.0 1.9 shard_map.58
  207.5 1.0 fusion.38
  208.5 3.7 %convolution_add_fusion = f32[65536,8]{0,1:T(8,128)} fusion(f32[65536,8]{0,1:T(8,128)S(1)} %fusion.38, bf16[8,65536]{1,0:T(8,128)(2,1)} %shard_map.56, f32[8,8]{1,0:T(8,128)} %shard_map.58), kind=kOutput, calls=%fused_computation | convolution fusion | flops 50855936 | bytes 5243136 | tf_op jit(solution)/shard_map/dot_general | solution.py:45
  (50 shorter events, 15.0 us)
Async XLA Ops:
  0.6 7.3 %copy-start.6 = (s32[1,8]{1,0:T(1,128)S(1)}, s32[1,8]{1,0:T(1,128)}, u32[]{:S(2)}) copy-start(s32[1,8]{1,0:T(1,128)} %param.9) | copy-start | bytes 100
  0.6 7.4 %copy-start.5 = (f32[64,8]{0,1:T(8,128)S(1)}, f32[64,8]{0,1:T(8,128)}, u32[]{:S(2)}) copy-start(f32[64,8]{0,1:T(8,128)} %param.8) | copy-start | bytes 6148
  66.6 22.0 %copy-start.2 = (f32[8,64,16]{2,1,0:T(8,128)S(1)}, f32[8,64,16]{2,1,0:T(8,128)}, u32[]{:S(2)}) copy-start(f32[8,64,16]{2,1,0:T(8,128)} %get-tuple-element.8) | copy-start | bytes 98308
  108.3 51.4 %copy-start = (f32[8,64,64]{2,1,0:T(8,128)S(1)}, f32[8,64,64]{2,1,0:T(8,128)}, u32[]{:S(2)}) copy-start(f32[8,64,64]{2,1,0:T(8,128)} %shard_map.51) | copy-start | bytes 393220
  113.9 47.5 %copy-start.3 = (f32[8,8]{1,0:T(8,128)S(1)}, f32[8,8]{1,0:T(8,128)}, u32[]{:S(2)}) copy-start(f32[8,8]{1,0:T(8,128)} %fusion.34.right_ref) | copy-start | bytes 772
  143.9 63.6 %copy-start.1 = (bf16[8,65536]{1,0:T(8,128)(2,1)S(1)}, bf16[8,65536]{1,0:T(8,128)(2,1)}, u32[]{:S(2)}) copy-start(bf16[8,65536]{1,0:T(8,128)(2,1)} %shard_map.52) | copy-start | bytes 3145732
  157.9 49.6 %copy-start.4 = (f32[8,8]{1,0:T(8,128)S(1)}, f32[8,8]{1,0:T(8,128)}, u32[]{:S(2)}) copy-start(f32[8,8]{1,0:T(8,128)} %shard_map.54) | copy-start | bytes 772

commit v3 on v2

--- a/solution.py
+++ b/solution.py
@@ -58,8 +58,8 @@
     )
 
 
-def gather_kernel(n, total_rows, scale, sums_ref, aux_ref, chosen_ref, full_ref, mean_ref, aux_out, rows_out, centered_ref,
-                  land, own, full, s1, r1, s2, r2, s3, r3, s4, r4, s5, r5, s6, r6, local):
+def gather_kernel(n, total_rows, scale, sums_ref, aux_ref, chosen_ref, full_ref, sketch_ref, aux_out, centered_out,
+                  mean_ref, rows_out, centered_ref, land, own, full, s1, r1, s2, r2, s3, r3, s4, r4, s5, r5, s6, r6, local):
     me, col = lax.axis_index("samp"), lax.axis_index("par")
     at = [lax.rem(me + k, n) for k in range(n)]
     back = [lax.rem(me + n - k, n) for k in range(n)]
@@ -137,6 +137,8 @@
             mean = mean_ref[j, :, pl.ds(inner, tile)]
             centered_ref[:, cols] = ((full[:, cols].astype(jnp.float32) - mean) * scale).astype(jnp.bfloat16)
 
+    put = pltpu.make_async_copy(centered_ref, centered_out, local.at[2])
+    put.start()
     if quad:
         for d in range(2):
             view = rows_out.at[beside[d], :, part[1 - d]]
@@ -175,6 +177,23 @@
         copy.wait_send()
     mine.wait()
     keep.wait()
+    sketch_ref[...] = jnp.zeros_like(sketch_ref)
+    count = n * chosen_ref.shape[0]
+
+    @pl.loop(0, n)
+    def _(j):
+        @pl.loop(0, slab // tile)
+        def _(t):
+            inner = pl.multiple_of(t * tile, tile)
+            cols = pl.ds(pl.multiple_of(j * slab + inner, tile), tile)
+            mean = mean_ref[j, :, pl.ds(inner, tile)]
+            rows = rows_out[:, :, cols].astype(jnp.float32).reshape(count, tile)
+            rows = ((rows - mean) * scale).astype(jnp.bfloat16)
+            sketch_ref[...] += lax.dot_general(
+                centered_ref[:, cols], rows, (((1,), (1,)), ((), ())), preferred_element_type=jnp.float32
+            )
+
+    put.wait()
 
 
 def gather_rows(sums, aux, chosen, full, n, total_rows, scale, ident):
@@ -184,14 +203,16 @@
     return pl.pallas_call(
         functools.partial(gather_kernel, n, total_rows, scale),
         out_shape=(
-            jax.ShapeDtypeStruct(sums.shape, jnp.float32),
+            jax.ShapeDtypeStruct((full.shape[0], n * chosen.shape[0]), jnp.float32),
             jax.ShapeDtypeStruct((n,) + aux.shape, jnp.float32),
-            jax.ShapeDtypeStruct((n,) + chosen.shape, chosen.dtype),
             jax.ShapeDtypeStruct(full.shape, full.dtype),
         ),
         in_specs=[vmem, vmem, vmem, pl.BlockSpec(memory_space=pl.ANY)],
-        out_specs=(vmem, vmem, vmem, vmem),
+        out_specs=(vmem, vmem, pl.BlockSpec(memory_space=pl.ANY)),
         scratch_shapes=[
+            pltpu.VMEM(sums.shape, jnp.float32),
+            pltpu.VMEM((n,) + chosen.shape, chosen.dtype),
+            pltpu.VMEM(full.shape, full.dtype),
             pltpu.VMEM(sums.shape, jnp.float32),
             pltpu.VMEM((1, slab), jnp.float32),
             pltpu.VMEM(full.shape, full.dtype),
@@ -354,11 +375,7 @@
     chosen = taken[:rank].astype(jnp.bfloat16)
     sums = taken[rank].reshape(n, 1, width // n)
     aux = jnp.concatenate([energies, picks.astype(jnp.float32).T], axis=1)
-    mean, aux_all, chosen_all, centered = gather_rows(sums, aux, chosen, log_derivs, n, n * rows, scale, 0)
-    mean = mean.reshape(1, width)
-    chosen_all = chosen_all.reshape(n * rank, width)
-    chosen_all = ((chosen_all.astype(jnp.float32) - mean) * scale).astype(jnp.bfloat16)
-    sketch_part = jnp.einsum("rc,kc->rk", centered, chosen_all, preferred_element_type=jnp.float32)
+    sketch_part, aux_all, centered = gather_rows(sums, aux, chosen, log_derivs, n, n * rows, scale, 0)
     sketch = sum_and_spread(sketch_part, n, p, 1).reshape(n * rows, n * rank)
     all_energies = aux_all[:, :, :count].reshape(n * rows, count)
     core_block = jnp.einsum(

time: 213 us -> 213 us (level)
  matrix products: 52.3 us -> 44.6 us
  Pallas kernels: 140 us -> 146 us
    dot_general x1 -> x0, matrix products: 8.75 us -> none  [body(): jnp.einsum('rc,kc->rk', centered, chosen_all, preferred_element_type=jnp....]
    pallas_call x1, Pallas kernels: 57.9 us -> 64.5 us  [gather_rows(): pl.pallas_call(functools.partial(gather_kernel, n, total_rows, scale), ou...]
where the time goes in v3:
time: 213 us; the launch traced here: 212 us
  Pallas kernels  146 us (69%)
  matrix products  44.6 us (21%)
  other arithmetic  15.5 us (7%)
  local copies, waits for them, and re-layouts  4.92 us (2%)
    pallas_call x1, Pallas kernels, gather_rows(): pl.pallas_call(functools.partial(gather_kernel, n, total_rows, scale), ou...  64.5 us
    pallas_call x2, Pallas kernels, reduce_all(): pl.pallas_call(functools.partial(reduce_kernel, n), out_shape=jax.ShapeDt...  45.6 us
    pallas_call x2, Pallas kernels, sum_and_spread(): pl.pallas_call(functools.partial(spread_kernel, n, p), out_shape=jax.Shap...  23.7 us
    dot_general x15, matrix products, hdot(): return jnp.dot(left, right, precision=lax.Precision.HIGHEST)  16.9 us
    dot_general x2, matrix products, body(): jnp.einsum('rv,rc->vc', rounded, centered, preferred_element_type=jnp.flo...  11.3 us
    pallas_call x1, Pallas kernels, tiny_sum(): pl.pallas_call(functools.partial(tiny_kernel, p), out_shape=jax.ShapeDtyp...  6.75 us
    dot_general x1, matrix products, body(): jnp.einsum('rc,vc->vr', centered, projected, preferred_element_type=jnp.f...  6.59 us
    another operation x3, other arithmetic, body(): factor = jnp.linalg.cholesky(damping * core_block + hdot(sketch.T, sketch))  6.52 us

profile of v3, /device:TPU:0, one launch (start us, length us, event | category | flops | bytes accessed | tf_op | source)
XLA Modules:
  0.0 212.1 jit_solution(10340738183449727721)
XLA Ops:
  1.4 4.6 %fusion.15 = f32[16,65536]{1,0:T(8,128)S(1)} fusion(bf16[64,65536]{1,0:T(8,128)(2,1)} %full_ref.1, pred[8,64]{1,0:T(8,128)(4,1)S(1)} %iota_compare_fusion.3), kind=kOutput, calls=%fused_computation.34 | convolution fusion | flops 134217728 | bytes 12583424 | tf_op jit(solution)/shard_map/dot_general | solution.py:374
  6.0 1.1 slice.34.chosen_ref
  8.7 64.5 %shard_map.50 = (f32[64,64]{1,0:T(8,128)}, f32[8,64,16]{2,1,0:T(8,128)}, bf16[64,65536]{1,0:T(8,128)(2,1)}) custom-call(f32[8,1,8192]{2,1,0:T(1,128)} %bitcast.91, f32[64,16]{1,0:T(8,128)} %copy.28.aux_ref, bf16[8,65536]{1,0:T(8,128)(2,1)} %slice.34.chosen_ref, bf16[64,65536]{1,0:T(8,128)(2,1)} %full_ref.1), custom_call_target="tpu_custom_call" | custom-call | tf_op jit(solution)/shard_map/pallas_call | solution.py:203
  73.2 13.3 %shard_map.51 = f32[8,64,64]{2,1,0:T(8,128)} custom-call(f32[64,64]{1,0:T(8,128)} %get-tuple-element.8.part_ref), custom_call_target="tpu_custom_call" | custom-call | tf_op jit(solution)/shard_map/pallas_call | solution.py:255
  86.5 1.7 fusion.1
  88.3 1.6 fusion
  90.0 5.8 %cholesky.18 = f32[64,64]{1,0:T(8,128)S(1)} custom-call(f32[64,64]{1,0:T(8,128)S(1)} %fusion.14), custom_call_target="Cholesky" | custom-call | tf_op jit(solution)/shard_map/jit(cholesky)/cholesky | solution.py:384
  97.2 4.9 %custom-call.12 = f32[1,64,64]{1,2,0:T(8,128)S(1)} custom-call(f32[1,64,64]{2,1,0:T(8,128)S(1)} %fusion.5), custom_call_target="InvertDiagBlocksLowerTriangular" | custom-call | tf_op jit(solution)/shard_map/triangular_solve/custom-call.2 | solution.py:21
  102.1 1.6 convolution_bitcast_fusion.1
  104.0 1.1 copy.35
  105.1 1.3 broadcast_multiply_fusion
  106.4 1.8 fusion.26.right_ref
  108.2 5.7 %convolution_convert_fusion.1.part_ref = bf16[8,65536]{1,0:T(8,128)(2,1)} fusion(bf16[64,65536]{1,0:T(8,128)(2,1)} %get-tuple-element.9, bf16[512,8]{0,1:T(8,128)(2,1)S(1)} %get-tuple-element.10, s32[]{:T(128)S(6)} %select_n.10), kind=kOutput, calls=%fused_computation.2 | convolution fusion | flops 67633152 | bytes 9439236 | tf_op jit(solution)/shard_map/rv,rc->vc/dot_general | solution.py:399
  113.8 23.3 %shard_map.52 = bf16[8,65536]{1,0:T(8,128)(2,1)} custom-call(bf16[8,65536]{1,0:T(8,128)(2,1)} %convolution_convert_fusion.1.part_ref), custom_call_target="tpu_custom_call" | custom-call | tf_op jit(solution)/shard_map/pallas_call | solution.py:320
  137.2 6.6 %fusion.29.part_ref = f32[8,64]{1,0:T(8,128)} fusion(bf16[8,65536]{1,0:T(8,128)(2,1)} %shard_map.52, bf16[64,65536]{1,0:T(8,128)(2,1)} %get-tuple-element.9), kind=kOutput, calls=%fused_computation.57 | convolution fusion | flops 67108864 | bytes 9439232 | tf_op jit(solution)/shard_map/rc,vc->vr/dot_general | solution.py:402
  143.8 10.4 %shard_map.53 = f32[8,8,64]{2,1,0:T(8,128)} custom-call(f32[8,64]{1,0:T(8,128)} %fusion.29.part_ref), custom_call_target="tpu_custom_call" | custom-call | tf_op jit(solution)/shard_map/pallas_call | solution.py:255
  155.9 1.9 shard_map.54
  162.0 1.9 shard_map.55
  164.8 5.6 %convolution_convert_fusion.part_ref = bf16[8,65536]{1,0:T(8,128)(2,1)} fusion(bf16[64,65536]{1,0:T(8,128)(2,1)} %get-tuple-element.9, f32[512,8]{0,1:T(8,128)S(1)} %convolution_add_fusion.1, s32[]{:T(128)S(6)} %select_n.10), kind=kOutput, calls=%fused_computation.1 | convolution fusion | flops 67633152 | bytes 9439236 | tf_op jit(solution)/shard_map/rv,rc->vc/dot_general | solution.py:399
  170.4 22.3 %shard_map.56 = bf16[8,65536]{1,0:T(8,128)(2,1)} custom-call(bf16[8,65536]{1,0:T(8,128)(2,1)} %convolution_convert_fusion.part_ref), custom_call_target="tpu_custom_call" | custom-call | tf_op jit(solution)/shard_map/pallas_call | solution.py:320
  192.7 2.9 %fusion.33.part_ref = f32[8,8]{1,0:T(8,128)} fusion(bf16[8,65536]{1,0:T(8,128)(2,1)} %shard_map.56), kind=kOutput, calls=%fused_computation.61 | convolution fusion | flops 8388608 | bytes 1048832 | tf_op jit(solution)/shard_map/uc,vc->uv/dot_general | solution.py:407
  195.6 6.8 %shard_map.57 = f32[8,8]{1,0:T(8,128)} custom-call(f32[8,8]{1,0:T(8,128)} %fusion.33.part_ref), custom_call_target="tpu_custom_call" | custom-call | tf_op jit(solution)/shard_map/pallas_call | solution.py:356
  203.9 1.9 shard_map.58
  208.4 3.7 %convolution_add_fusion = f32[65536,8]{0,1:T(8,128)} fusion(f32[65536,8]{0,1:T(8,128)S(1)} %fusion.30, bf16[8,65536]{1,0:T(8,128)(2,1)} %shard_map.56, f32[8,8]{1,0:T(8,128)} %shard_map.58), kind=kOutput, calls=%fused_computation | convolution fusion | flops 50855936 | bytes 5243136 | tf_op jit(solution)/shard_map/dot_general | solution.py:45
  (47 shorter events, 15.0 us)
Async XLA Ops:
  0.6 7.3 %copy-start.5 = (s32[1,8]{1,0:T(1,128)S(1)}, s32[1,8]{1,0:T(1,128)}, u32[]{:S(2)}) copy-start(s32[1,8]{1,0:T(1,128)} %param.9) | copy-start | bytes 100
  0.6 7.4 %copy-start.4 = (f32[64,8]{0,1:T(8,128)S(1)}, f32[64,8]{0,1:T(8,128)}, u32[]{:S(2)}) copy-start(f32[64,8]{0,1:T(8,128)} %param.8) | copy-start | bytes 6148
  108.2 51.4 %copy-start = (f32[8,64,64]{2,1,0:T(8,128)S(1)}, f32[8,64,64]{2,1,0:T(8,128)}, u32[]{:S(2)}) copy-start(f32[8,64,64]{2,1,0:T(8,128)} %shard_map.51) | copy-start | bytes 393220
  113.8 47.5 %copy-start.2 = (f32[8,8]{1,0:T(8,128)S(1)}, f32[8,8]{1,0:T(8,128)}, u32[]{:S(2)}) copy-start(f32[8,8]{1,0:T(8,128)} %fusion.26.right_ref) | copy-start | bytes 772
  143.8 63.6 %copy-start.1 = (bf16[8,65536]{1,0:T(8,128)(2,1)S(1)}, bf16[8,65536]{1,0:T(8,128)(2,1)}, u32[]{:S(2)}) copy-start(bf16[8,65536]{1,0:T(8,128)(2,1)} %shard_map.52) | copy-start | bytes 3145732
  157.8 49.6 %copy-start.3 = (f32[8,8]{1,0:T(8,128)S(1)}, f32[8,8]{1,0:T(8,128)}, u32[]{:S(2)}) copy-start(f32[8,8]{1,0:T(8,128)} %shard_map.54) | copy-start | bytes 772
